TPU v7x, 32 devices: a whole 2x2x4 slice. The times are simulated.
32 devices in a mesh: dp: 8 (over z, y), mp: 4 (over x, core).
Axes of the slice: x: 2, y: 2, z: 4, core: 2. Of those that a mesh axis runs over, the one named last changes fastest.
Arguments:
- clean: bfloat16 [16, 128, 2432], P('dp'), may hold values from -6 to 6
- noise: bfloat16 [16, 128, 2432], P('dp'), may hold values from -6 to 6
- modulation: float32 [16, 7296], P('dp'), may hold values from -3 to 3
- strata: int32 [16], P('dp'), may hold values from 0 to 63
- up_weight: bfloat16 [2432, 5376], P(None, 'mp'), may hold values from -0.125 to 0.125
- down_weight: bfloat16 [5376, 2432], P('mp'), may hold values from -0.078125 to 0.078125
Outputs:
- up_gradient: float32 [5376, 2432], P(('mp', 'dp'))
- loss_value: float32 [], replicated
All inputs are finite; a program needn't handle non-finite values.
Results may differ from a plain program's by a relative error of at most 0.008.
Values may be sent and summed in bfloat16 or wider, within the bound.
A program may use at most 128 MiB of HBM per device.

v0:
```python
import math

import jax
import jax.numpy as jnp
from jax import lax
from jax.sharding import PartitionSpec as P

STRATA = 64


loss_scale = 1048576.0


def stratum_weights(strata):
    quantile = (strata.astype(jnp.float32) + 0.5) / STRATA
    levels = math.sqrt(2.0) * lax.erf_inv(2.0 * quantile - 1.0)
    fraction = jax.nn.sigmoid(levels)
    weight = jnp.exp(-0.5 * levels * levels) / (
        math.sqrt(2.0 * math.pi) * fraction * (1.0 - fraction)
    )
    return (fraction, weight)


def modulate(clean, noise, modulation, fraction):
    features = clean.shape[-1]
    anchor = clean.astype(jnp.float32)
    drift_field = noise.astype(jnp.float32)
    mix_frac = fraction[:, None, None]
    noisy_field = (1.0 - mix_frac) * anchor + mix_frac * drift_field
    target = drift_field - anchor
    row_mean = jnp.mean(noisy_field, -1, keepdims=True)
    centred = noisy_field - row_mean
    variance = jnp.mean(centred * centred, -1, keepdims=True)
    normed = centred * lax.rsqrt(variance + 1e-06)
    shifts = modulation[:, None, :features]
    scales = modulation[:, None, features : 2 * features]
    modulated = (normed * (1.0 + scales) + shifts).astype(jnp.bfloat16)
    return (noisy_field, target, modulated, modulation[:, 2 * features :])


def gelu_tanh(values):
    return jax.nn.gelu(values, approximate=True)


def local(clean, noise, modulation, strata, up_weight, down_weight):
    samples_here, rows_per, features = clean.shape
    tokens_here = samples_here * rows_per
    fraction, weight = stratum_weights(strata)
    noisy_field, target, modulated, gate_values = modulate(clean, noise, modulation, fraction)
    flat_rows = modulated.reshape(tokens_here, features)
    flat_noisy = noisy_field.reshape(tokens_here, features)
    flat_target = target.reshape(tokens_here, features)
    local_total = jnp.sum(weight)
    grand_total = lax.psum(local_total, "dp")
    preact = jnp.dot(flat_rows, up_weight, preferred_element_type=jnp.float32)
    hidden = gelu_tanh(preact).astype(jnp.bfloat16)
    partial_value = jnp.dot(hidden, down_weight, preferred_element_type=jnp.float32)
    share_rows = tokens_here // lax.axis_size("mp")
    first_row = lax.axis_index("mp") * share_rows
    sample_range = jnp.arange(samples_here, dtype=jnp.int32)
    owners = (first_row + jnp.arange(share_rows, dtype=jnp.int32)) // rows_per
    picker = (owners[:, None] == sample_range[None, :]).astype(jnp.float32)
    own_weight = jnp.dot(picker, weight, precision=lax.Precision.HIGHEST)
    output = lax.psum(partial_value.astype(jnp.bfloat16), "mp").astype(jnp.float32)
    sample_ids = jnp.arange(tokens_here, dtype=jnp.int32) // rows_per
    full_picker = (sample_ids[:, None] == sample_range[None, :]).astype(jnp.float32)
    gate_rows = jnp.dot(full_picker, gate_values, precision=lax.Precision.HIGHEST)
    row_weight = jnp.dot(full_picker, weight, precision=lax.Precision.HIGHEST)
    errors = flat_noisy + gate_rows * output - flat_target
    row_squares = jnp.sum(errors * errors, 1)
    own_squares = lax.dynamic_slice_in_dim(row_squares, first_row, share_rows, 0)
    loss_local = jnp.sum(own_weight * own_squares) / (rows_per * features)
    factor = loss_scale * 2.0 / (grand_total * rows_per * features)
    slopes = (factor * row_weight[:, None] * gate_rows * errors).astype(jnp.bfloat16)
    hidden_slope = lax.dot_general(
        slopes, down_weight, (((1,), (1,)), ((), ())), preferred_element_type=jnp.float32
    )
    unused, pullback = jax.vjp(gelu_tanh, preact)
    pre_slope = pullback(hidden_slope)[0].astype(jnp.bfloat16)
    gradient = lax.psum_scatter(
        lax.dot_general(
            pre_slope, flat_rows, (((0,), (0,)), ((), ())), preferred_element_type=jnp.float32
        ),
        "dp",
        scatter_dimension=0,
        tiled=True,
    )
    loss_sum = lax.psum(loss_local, ("dp", "mp"))
    return (gradient, loss_sum / grand_total)


def solution(mesh):
    return jax.shard_map(
        local,
        mesh=mesh,
        in_specs=(
            P("dp", None, None),
            P("dp", None, None),
            P("dp", None),
            P("dp"),
            P(None, "mp"),
            P("mp", None),
        ),
        out_specs=(P(("mp", "dp"), None), P()),
        check_vma=False,
    )
```

profile of v0, /device:TPU:0, one launch (start us, length us, event | category | flops | bytes accessed | tf_op | source)
XLA Modules:
  0.0 309.5 jit_solution(266357300899016606)
XLA Ops:
  7.2 0.0 all-reduce.3.cloned.1.call-start
  7.2 1.3 fusion.45
  8.5 0.8 slice_add_fusion
  9.3 0.0 copy-start.2
  9.3 4.4 %fusion.46 = (f32[2,128]{1,0:T(2,128)S(1)}, f32[2,128,2432]{2,1,0:T(8,128)S(1)}, f32[2,128,2432]{2,1,0:T(8,128)}) fusion(bf16[2,128,2432]{2,1,0:T(8,128)(2,1)} %param.7, f32[2]{0:T(128)S(1)} %get-tuple-element.6, bf16[2,128,2432]{2,1,0:T(8,128)(2,1)} %param.6, f32[2]{0:T(128)S(1)} %broadcast_subtract_fusion), kind=kLoop, calls=%fused_computation.79 | loop fusion | flops 4357888 | bytes 7472144 | tf_op jit(solution)/shard_map/reduce_sum | solution.py:31
  13.8 0.4 multiply_reduce_fusion.1
  14.2 0.0 slice-start
  14.2 0.6 add_convert_fusion
  14.8 0.0 copy-start
  14.8 0.0 copy-done.2
  14.8 0.0 slice-start.1
  14.9 2.0 fusion.48
  16.9 0.0 copy-done
  16.9 0.0 copy-start.1
  16.9 1.1 copy-done.1
  18.0 0.0 slice-done
  18.0 0.0 slice-done.1
  18.0 3.3 %convolution_convert_fusion = bf16[256,2432]{1,0:T(8,128)(2,1)} fusion(bf16[1344,2432]{1,0:T(8,128)(2,1)S(1)} %bitcast.29, f32[256,1344]{0,1:T(8,128)S(1)} %fusion.48), kind=kOutput, calls=%fused_computation | convolution fusion | flops 1677246464 | bytes 9158656 | tf_op jit(solution)/shard_map/dot_general | solution.py:57
  21.3 0.0 all-reduce.3.cloned.1.call-update
  21.3 0.0 reduce-scatter.4.cloned.1.call-start
  21.4 24.0 %psum.21 = f32[]{:T(128)} all-reduce(f32[]{:T(128)} %get-tuple-element.4), channel_id=1, replica_groups=mesh['dp'=8,'mp'=4] {'dp'}, use_global_device_ids=true, to_apply=%region_1.0 | all-reduce | flops 1 | bytes 8 | tf_op jit(solution)/shard_map/psum | solution.py:54
  46.1 0.2 fusion.26
  46.3 16.2 %all-reduce.3.cloned.1.call-done = bf16[256,2432]{1,0:T(8,128)(2,1)} async-done(((bf16[256,2432]{1,0:T(8,128)(2,1)}), bf16[256,2432]{1,0:T(8,128)(2,1)}) %all-reduce.3.cloned.1.call-update) | async-done | bytes 1245200 | tf_op jit(solution)/shard_map/psum | solution.py:64
  62.5 5.9 %multiply_reduce_fusion = (f32[256]{0:T(256)S(1)}, f32[256,2432]{1,0:T(8,128)}, f32[256,2432]{1,0:T(8,128)}) fusion(f32[2,128,2432]{2,1,0:T(8,128)} %get-tuple-element.9, bf16[256,2432]{1,0:T(8,128)(2,1)} %all-reduce.3.cloned.1.call-done, f32[2,128,2432]{2,1,0:T(8,128)S(1)} %get-tuple-element.8, f32[2,7296]{1,0:T(2,128)} %param.8, s32[256]{0:T(256)S(1)} %and_select_fusion.1), kind=kOutput, calls=%fused_computation.7 | convolution fusion | flops 18678016 | bytes 11228160 | tf_op jit(solution)/shard_map/dot_general | solution.py:67
  68.4 17.5 %fusion.9 = f32[1344,2432]{1,0:T(8,128)} fusion(bf16[256,2432]{1,0:T(8,128)(2,1)} %bitcast.31, f32[256,1344]{0,1:T(8,128)} %copy-done.1, bf16[1344,2432]{1,0:T(8,128)(2,1)} %param.11, f32[256,2432]{1,0:T(8,128)} %get-tuple-element.3, f32[256,2432]{1,0:T(8,128)} %get-tuple-element.12, f32[256]{0:T(256)S(1)} %broadcast_multiply_fusion.1), kind=kOutput, calls=%fused_computation.22 | convolution fusion | flops 3355803648 | bytes 27214848 | tf_op jit(solution)/shard_map/dot_general | solution.py:81
  85.9 0.0 reduce-scatter.4.cloned.1.call-update
  85.9 0.8 fusion.24
  87.3 44.6 %psum.23 = f32[]{:T(128)} all-reduce(f32[]{:T(128)S(6)} %div.55), channel_id=1, replica_groups=mesh['dp'=8,'mp'=4] {'dp','mp'}, use_global_device_ids=true, to_apply=%region_8.9 | all-reduce | flops 1 | bytes 8 | tf_op jit(solution)/shard_map/psum | solution.py:88
  133.2 168.3 %reduce-scatter.4.cloned.1.call-done = f32[168,2432]{1,0:T(8,128)} async-done(((f32[1344,2432]{1,0:T(8,128)}), f32[168,2432]{1,0:T(8,128)}) %reduce-scatter.4.cloned.1.call-update) | async-done | bytes 1634320
  (7 shorter events, 0.0 us)
Async XLA Ops:
  7.2 55.3 %all-reduce.3.cloned.1.call-start = ((), (), s32[]{:S(2)}) async-start(), calls=%async_computation.1 | async-start | bytes 2490368 | tf_op jit(solution)/shard_map/psum | solution.py:64
  9.3 5.5 %copy-start.2 = (bf16[2432,1344]{0,1:T(8,128)(2,1)S(1)}, bf16[2432,1344]{0,1:T(8,128)(2,1)}, u32[]{:S(2)}) copy-start(bf16[2432,1344]{0,1:T(8,128)(2,1)} %param.10) | copy-start | bytes 19611652
  14.2 3.8 %slice-start = ((s8[6537216]{0:T(1024)(128)(4,1)}), s8[4194304]{0:T(1024)(128)(4,1)S(1)}, s32[]{:S(2)}) async-start(s8[6537216]{0:T(1024)(128)(4,1)} %bitcast.28), calls=%async_computation.3 | async-start | bytes 8388608
  14.8 2.1 copy-start
  14.8 3.1 %slice-start.1 = ((s8[6537216]{0:T(1024)(128)(4,1)}), s8[2342912]{0:T(1024)(128)(4,1)S(1)}, s32[]{:S(2)}) async-start(s8[6537216]{0:T(1024)(128)(4,1)} %bitcast.28), calls=%async_computation.4 | async-start | bytes 4685824
  16.9 1.1 copy-start.1
  21.3 280.2 %reduce-scatter.4.cloned.1.call-start = ((), (), s32[]{:S(2)}) async-start(), calls=%async_computation.2 | async-start | bytes 14708736
Sparse Core Ops, SparseCore 0:
  21.5 40.9 all-reduce.2
  86.0 215.4 reduce-scatter.3
where the time goes:
time: 310 us; the launch traced here: 309 us
  waiting for transfers between devices  185 us (60%)
  blocking collectives  68.6 us (22%)
  matrix products  29.8 us (10%)
  between operations  17.8 us (6%)
  other arithmetic  7.59 us (2%)
    unnamed x3, waiting for transfers between devices  168 us
    psum x1, blocking collectives, local(): loss_sum = lax.psum(loss_local, ('dp', 'mp'))  44.6 us
    psum x1, blocking collectives, local(): grand_total = lax.psum(local_total, 'dp')  24 us
    dot_general x1, matrix products, local(): lax.dot_general(pre_slope, flat_rows, (((0,), (0,)), ((), ())), preferred...  17.5 us
    psum x1, waiting for transfers between devices, local(): lax.psum(partial_value.astype(jnp.bfloat16), 'mp').astype(jnp.float32)  16.2 us
  transfers between devices with their start and end apart: 2, of which 2 were waited for; matrix products, arithmetic and copies ran while one was open for 0% of the time, Pallas kernels for 0%

commit v1 on v0

--- a/solution.py
+++ b/solution.py
@@ -42,7 +42,7 @@
     return jax.nn.gelu(values, approximate=True)
 
 
-def local(clean, noise, modulation, strata, up_weight, down_weight):
+def local_scatter(clean, noise, modulation, strata, up_weight, down_weight):
     samples_here, rows_per, features = clean.shape
     tokens_here = samples_here * rows_per
     fraction, weight = stratum_weights(strata)
@@ -89,6 +89,48 @@
     return (gradient, loss_sum / grand_total)
 
 
+GATHER_LIMIT_BYTES = 33554432
+
+
+def local_gather(clean, noise, modulation, strata, up_weight, down_weight):
+    samples_here, rows_per, features = clean.shape
+    tokens_here = samples_here * rows_per
+    fraction, weight = stratum_weights(strata)
+    noisy_field, target, modulated, gate_values = modulate(clean, noise, modulation, fraction)
+    flat_rows = modulated.reshape(tokens_here, features)
+    every_row = lax.all_gather(flat_rows, "dp", axis=0, tiled=True)
+    preact = jnp.dot(flat_rows, up_weight, preferred_element_type=jnp.float32)
+    hidden = gelu_tanh(preact).astype(jnp.bfloat16)
+    partial_value = jnp.dot(hidden, down_weight, preferred_element_type=jnp.float32)
+    output = lax.psum(partial_value.astype(jnp.bfloat16), "mp").astype(jnp.float32)
+    output = output.reshape(samples_here, rows_per, features)
+    gates = gate_values[:, None, :]
+    errors = noisy_field + gates * output - target
+    squares = jnp.sum(errors * errors, axis=(1, 2)) / (rows_per * features)
+    factor = loss_scale * 2.0 / (rows_per * features)
+    slopes = (factor * weight[:, None, None] * gates * errors).astype(jnp.bfloat16)
+    hidden_slope = lax.dot_general(
+        slopes.reshape(tokens_here, features),
+        down_weight,
+        (((1,), (1,)), ((), ())),
+        preferred_element_type=jnp.float32,
+    )
+    unused, pullback = jax.vjp(gelu_tanh, preact)
+    pre_slope = pullback(hidden_slope)[0].astype(jnp.bfloat16)
+    own_slope = lax.all_to_all(pre_slope, "dp", split_axis=1, concat_axis=0, tiled=True)
+    sums = lax.psum(jnp.stack([jnp.sum(weight * squares), jnp.sum(weight)]), "dp")
+    gradient = lax.dot_general(
+        own_slope, every_row, (((0,), (0,)), ((), ())), preferred_element_type=jnp.float32
+    )
+    return (gradient / sums[1], sums[0] / sums[1])
+
+
+def local(clean, *others):
+    gathered = lax.axis_size("dp") * clean.size * clean.dtype.itemsize
+    body = local_gather if gathered <= GATHER_LIMIT_BYTES else local_scatter
+    return body(clean, *others)
+
+
 def solution(mesh):
     return jax.shard_map(
         local,

time: 310 us -> 200 us (0.65)
  waiting for transfers between devices: 185 us -> 104 us
  blocking collectives: 68.6 us -> 32.5 us
  starting transfers between devices: 0.08 us -> 5.58 us
  other arithmetic: 7.59 us -> 11.9 us
  matrix products: 29.8 us -> 25.9 us
    unnamed x3 -> x2, waiting for transfers between devices: 168 us -> 0.54 us
    all_gather x0 -> x1, waiting for transfers between devices: none -> 63.1 us  [local_gather(): every_row = lax.all_gather(flat_rows, 'dp', axis=0, tiled=True)]
    psum x2 -> x1, blocking collectives: 68.6 us -> 32.5 us  [local_gather(): lax.psum(jnp.stack([jnp.sum(weight * squares), jnp.sum(weight)]), 'dp')]
    psum x1, waiting for transfers between devices: 16.2 us -> 40.6 us  [local_gather(): lax.psum(partial_value.astype(jnp.bfloat16), 'mp').astype(jnp.float32)]
    all_to_all x0 -> x1, starting transfers between devices: none -> 5.5 us  [local_gather(): lax.all_to_all(pre_slope, 'dp', split_axis=1, concat_axis=0, tiled=True)]
    dot_general x6 -> x4, matrix products: 29.8 us -> 25.9 us  [the longest x1 7.51 us: local_gather(): lax.dot_general(own_slope, every_row, (((0,), (0,)), ((), ())), preferred...]
  transfers between devices with their start and end apart: 2 -> 3, of which waited for: 2 -> 2; matrix products, arithmetic and copies ran while one was open for 0% -> 6% of each run, Pallas kernels for 0% -> 0%
where the time goes in v1:
time: 200 us; the launch traced here: 199 us
  waiting for transfers between devices  104 us (52%)
  blocking collectives  32.5 us (16%)
  matrix products  25.9 us (13%)
  between operations  18 us (9%)
  other arithmetic  11.9 us (6%)
  starting transfers between devices  5.58 us (3%)
    all_gather x1, waiting for transfers between devices, local_gather(): every_row = lax.all_gather(flat_rows, 'dp', axis=0, tiled=True)  63.1 us
    psum x1, waiting for transfers between devices, local_gather(): lax.psum(partial_value.astype(jnp.bfloat16), 'mp').astype(jnp.float32)  40.6 us
    psum x1, blocking collectives, local_gather(): lax.psum(jnp.stack([jnp.sum(weight * squares), jnp.sum(weight)]), 'dp')  32.5 us
    dot_general x1, matrix products, local_gather(): lax.dot_general(own_slope, every_row, (((0,), (0,)), ((), ())), preferred...  7.51 us
    dot_general x1, matrix products, local_gather(): jnp.dot(hidden, down_weight, preferred_element_type=jnp.float32)  6.74 us
    dot_general x1, matrix products, local_gather(): lax.dot_general(slopes.reshape(tokens_here, features), down_weight, (((1,...  6.4 us
    all_to_all x1, starting transfers between devices, local_gather(): lax.all_to_all(pre_slope, 'dp', split_axis=1, concat_axis=0, tiled=True)  5.5 us
    dot_general x1, matrix products, local_gather(): preact = jnp.dot(flat_rows, up_weight, preferred_element_type=jnp.float32)  5.27 us
  transfers between devices with their start and end apart: 3, of which 2 were waited for; matrix products, arithmetic and copies ran while one was open for 6% of the time, Pallas kernels for 0%

profile of v1, /device:TPU:0, one launch (start us, length us, event | category | flops | bytes accessed | tf_op | source)
XLA Modules:
  0.0 199.1 jit_solution(13878708809790804835)
XLA Ops:
  8.0 0.0 copy-start.1
  8.0 0.0 copy-start
  8.0 0.0 all-reduce.2.cloned.1.call-start
  8.1 0.9 broadcast_subtract_fusion
  8.9 0.0 copy-start.3
  8.9 2.3 %fusion.2 = f32[2,128]{1,0:T(2,128)S(1)} fusion(bf16[2,128,2432]{2,1,0:T(8,128)(2,1)} %param.7, bf16[2,128,2432]{2,1,0:T(8,128)(2,1)} %param.6, f32[2]{0:T(128)S(1)} %get-tuple-element.6, f32[2]{0:T(128)S(1)} %get-tuple-element.5), kind=kLoop, calls=%fused_computation.11 | loop fusion | flops 3735296 | bytes 2491408 | tf_op jit(solution)/shard_map/reduce_sum | solution.py:31
  11.2 0.0 copy-done.1
  11.3 0.0 copy-done
  11.3 0.8 multiply_reduce_fusion.1
  12.1 0.0 copy-done.3
  12.1 2.4 %add_convert_fusion = bf16[2,128,2432]{2,1,0:T(8,128)(2,1)} fusion(bf16[2,128,2432]{2,1,0:T(8,128)(2,1)S(1)} %copy-done, bf16[2,128,2432]{2,1,0:T(8,128)(2,1)S(1)} %copy-done.1, f32[2,2432]{1,0:T(2,128)S(1)} %get-tuple-element.9, f32[2,2432]{1,0:T(2,128)S(1)} %get-tuple-element.10, f32[2,128]{1,0:T(2,128)S(1)} %add_rsqrt_fusion, ...), kind=kLoop, calls=%fused_computation.9 | loop fusion | flops 6225920 | bytes 3776528 | tf_op jit(solution)/shard_map/convert_element_type | solution.py:37
  14.5 5.3 %fusion.22 = f32[256,1344]{0,1:T(8,128)S(1)} fusion(bf16[256,2432]{1,0:T(8,128)(2,1)} %bitcast.18, bf16[2432,1344]{0,1:T(8,128)(2,1)} %param.10), kind=kOutput, calls=%fused_computation.48 | convolution fusion | flops 1673527296 | bytes 9158656 | tf_op jit(solution)/shard_map/dot_general | solution.py:102
  19.8 0.0 copy-start.4
  19.8 6.7 %convolution_convert_fusion = bf16[256,2432]{1,0:T(8,128)(2,1)} fusion(bf16[1344,2432]{1,0:T(8,128)(2,1)} %param.11, f32[256,1344]{0,1:T(8,128)S(1)} %fusion.22), kind=kOutput, calls=%fused_computation | convolution fusion | flops 1677246464 | bytes 9158656 | tf_op jit(solution)/shard_map/dot_general | solution.py:104
  26.5 0.0 copy-done.4
  26.5 0.0 all-reduce.2.cloned.1.call-update
  26.5 0.0 all-gather.2.cloned.1.call-start
  26.6 0.5 all-gather.2.cloned.1.call-update
  27.1 40.6 %all-reduce.2.cloned.1.call-done = bf16[2,128,2432]{2,1,0:T(8,128)(2,1)} async-done(((bf16[2,128,2432]{2,1,0:T(8,128)(2,1)}), bf16[2,128,2432]{2,1,0:T(8,128)(2,1)}) %all-reduce.2.cloned.1.call-update) | async-done | bytes 1245200 | tf_op jit(solution)/shard_map/psum | solution.py:105
  67.7 0.0 copy-start.2
  67.7 2.5 %multiply_reduce_fusion = f32[2]{0:T(128)S(1)} fusion(bf16[2,128,2432]{2,1,0:T(8,128)(2,1)} %all-reduce.2.cloned.1.call-done, f32[2,2432]{1,0:T(2,128)S(1)} %get-tuple-element.8, bf16[2,128,2432]{2,1,0:T(8,128)(2,1)S(1)} %copy-done, f32[2]{0:T(128)S(1)} %get-tuple-element.6, bf16[2,128,2432]{2,1,0:T(8,128)(2,1)S(1)} %copy-done.1, f32[2]{0:T(128)S(1)} %get-tuple-element.5), kind=kLoop, calls=%fused_computation.7 | loop fusion | flops 7471102 | bytes 3755032 | tf_op jit(solution)/shard_map/reduce_sum | solution.py:109
  70.2 0.6 multiply_reduce_fusion.2
  70.8 0.1 broadcast_multiply_fusion
  70.9 0.0 copy-done.2
  70.9 0.0 copy-start.5
  70.9 1.0 multiply_convert_fusion
  71.9 0.3 copy-done.5
  72.3 6.4 %fusion.9 = bf16[256,1344]{0,1:T(8,128)(2,1)} fusion(f32[256,1344]{0,1:T(8,128)S(1)} %copy-done.5, bf16[256,2432]{1,0:T(8,128)(2,1)S(1)} %bitcast.22, bf16[1344,2432]{1,0:T(8,128)(2,1)} %param.11), kind=kOutput, calls=%fused_computation.20 | convolution fusion | flops 1680408576 | bytes 9846784 | tf_op jit(solution)/shard_map/dot_general | solution.py:112
  78.7 5.5 %all-to-all-start = ((bf16[256,8,168]{0,2,1:T(8,128)(2,1)}), bf16[256,8,168]{0,2,1:T(8,128)(2,1)S(1)}, u32[]{:S(2)}, u32[]{:S(2)}) async-start(bf16[256,8,168]{0,2,1:T(8,128)(2,1)} %bitcast.3), calls=%async_computation | async-start | bytes 1376256 | tf_op jit(solution)/shard_map/all_to_all | solution.py:120
  84.2 1.3 pad_maximum_fusion
  85.5 32.5 %psum.15 = f32[2]{0:T(128)S(1)} all-reduce(f32[2]{0:T(128)S(1)} %pad_maximum_fusion), channel_id=1, replica_groups=mesh['dp'=8,'mp'=4] {'dp'}, use_global_device_ids=true, to_apply=%region_6.0 | all-reduce | flops 2 | bytes 16 | tf_op jit(solution)/shard_map/psum | solution.py:121
  118.0 0.6 fusion.21
  119.8 0.0 all-to-all-done
  119.8 0.1 copy.10
  119.9 63.1 %all-gather.2.cloned.1.call-done = bf16[2048,2432]{1,0:T(8,128)(2,1)} async-done(((bf16[256,2432]{1,0:T(8,128)(2,1)}), bf16[2048,2432]{1,0:T(8,128)(2,1)}) %all-gather.2.cloned.1.call-update) | async-done | bytes 9961488 | tf_op jit(solution)/shard_map/all_gather | solution.py:101
  183.0 7.5 %convolution_divide_fusion = f32[168,2432]{1,0:T(8,128)} fusion(bf16[2048,168]{0,1:T(8,128)(2,1)S(1)} %bitcast.23, bf16[2048,2432]{1,0:T(8,128)(2,1)} %all-gather.2.cloned.1.call-done, f32[]{:T(128)} %bitcast.7), kind=kOutput, calls=%fused_computation.1 | convolution fusion | flops 1673935872 | bytes 12283908 | tf_op jit(solution)/shard_map/dot_general | solution.py:122
  (4 shorter events, 0.0 us)
Async XLA Ops:
  8.0 3.2 %copy-start.1 = (bf16[2,128,2432]{2,1,0:T(8,128)(2,1)S(1)}, bf16[2,128,2432]{2,1,0:T(8,128)(2,1)}, u32[]{:S(2)}) copy-start(bf16[2,128,2432]{2,1,0:T(8,128)(2,1)} %param.6) | copy-start | bytes 3735556
  8.0 3.2 %copy-start = (bf16[2,128,2432]{2,1,0:T(8,128)(2,1)S(1)}, bf16[2,128,2432]{2,1,0:T(8,128)(2,1)}, u32[]{:S(2)}) copy-start(bf16[2,128,2432]{2,1,0:T(8,128)(2,1)} %param.7) | copy-start | bytes 3735556
  8.0 59.7 %all-reduce.2.cloned.1.call-start = ((), (), s32[]{:S(2)}) async-start(), calls=%async_computation.1 | async-start | bytes 2490368 | tf_op jit(solution)/shard_map/psum | solution.py:105
  8.9 3.1 %copy-start.3 = (f32[2,7296]{1,0:T(2,128)S(1)}, f32[2,7296]{1,0:T(2,128)}, u32[]{:S(2)}) copy-start(f32[2,7296]{1,0:T(2,128)} %param.8) | copy-start | bytes 175108
  19.8 6.8 %copy-start.4 = (f32[256,1344]{0,1:T(8,128)}, f32[256,1344]{0,1:T(8,128)S(1)}, u32[]{:S(2)}) copy-start(f32[256,1344]{0,1:T(8,128)S(1)} %fusion.22) | copy-start | bytes 4128772
  26.5 156.5 %all-gather.2.cloned.1.call-start = ((), (), s32[]{:S(2)}) async-start(), calls=%async_computation.2 | async-start | bytes 11206656 | tf_op jit(solution)/shard_map/all_gather | solution.py:101
  67.7 3.2 %copy-start.2 = (bf16[2,128,2432]{2,1,0:T(8,128)(2,1)S(1)}, bf16[2,128,2432]{2,1,0:T(8,128)(2,1)}, u32[]{:S(2)}) copy-start(bf16[2,128,2432]{2,1,0:T(8,128)(2,1)} %all-reduce.2.cloned.1.call-done) | copy-start | bytes 3735556
  70.9 1.3 copy-start.5
  78.7 41.2 %all-to-all-start = ((bf16[256,8,168]{0,2,1:T(8,128)(2,1)}), bf16[256,8,168]{0,2,1:T(8,128)(2,1)S(1)}, u32[]{:S(2)}, u32[]{:S(2)}) async-start(bf16[256,8,168]{0,2,1:T(8,128)(2,1)} %bitcast.3), calls=%async_computation | async-start | bytes 1376256 | tf_op jit(solution)/shard_map/all_to_all | solution.py:120
Sparse Core Ops, SparseCore 0:
  26.7 40.9 all-reduce.1
Sparse Core Ops, SparseCore 1:
  29.2 153.7 all-gather.1

commit v2 on v1

--- a/solution.py
+++ b/solution.py
@@ -1,8 +1,11 @@
+import functools
 import math
 
 import jax
 import jax.numpy as jnp
 from jax import lax
+from jax.experimental import pallas as pl
+from jax.experimental.pallas import tpu as pltpu
 from jax.sharding import PartitionSpec as P
 
 STRATA = 64
@@ -125,15 +128,434 @@
     return (gradient / sums[1], sums[0] / sums[1])
 
 
-def local(clean, *others):
+MESH = pl.DeviceIdType.MESH
+CHUNK = 16
+LANES = 128
+CORES = 2
+
+
+def gelu_slope(x):
+    k = math.sqrt(2.0 / math.pi)
+    t = jnp.tanh(k * (x + 0.044715 * (x * x * x)))
+    return 0.5 * (1.0 + t) + 0.5 * x * (1.0 - t * t) * (k * (1.0 + 3.0 * 0.044715 * x * x))
+
+
+def step_kernel(
+    sizes,
+    frac_ref,
+    weight_ref,
+    clean_ref,
+    noise_ref,
+    modulation_ref,
+    up_hbm,
+    down_hbm,
+    grad_ref,
+    sums_ref,
+    up,
+    down,
+    rows_all,
+    preact,
+    slope_t,
+    hidden,
+    part_out,
+    part_in,
+    part_own,
+    chip_sum,
+    slopes,
+    pre_out,
+    pre_in,
+    core_tile,
+    all_tile,
+    load_sem,
+    rows_send,
+    rows_recv,
+    part_sem,
+    chip_send,
+    chip_recv,
+    slopes_sem,
+    core_sem,
+    pre_send,
+    pre_recv,
+    tile_send,
+    tile_recv,
+):
+    nz, ny, nx, rows_per = sizes
+    ndp = nz * ny
+    samples, features = clean_ref.shape[0] // rows_per, clean_ref.shape[1]
+    units = up.shape[1]
+    half = clean_ref.shape[0] // CORES
+    share = units // ndp
+    kinds = 3 + (ny - 1)
+    me, group = lax.axis_index("dp"), lax.axis_index("mp")
+    z, y = me // ny, lax.rem(me, ny)
+    x, core = group // CORES, lax.rem(group, CORES)
+    mate = (me, x * CORES + 1 - core)
+    own_rows = pl.ds(pl.multiple_of(core * half, half), half)
+    mate_rows = pl.ds(pl.multiple_of((1 - core) * half, half), half)
+
+    load_up = pltpu.make_async_copy(up_hbm, up, load_sem.at[0])
+    load_down = pltpu.make_async_copy(down_hbm, down, load_sem.at[1])
+    load_up.start()
+    load_down.start()
+
+    others = [(lax.rem(me + k, ndp), group) for k in range(1, ndp)]
+    across = [lax.rem(x + k, nx) for k in range(1, nx)]
+    barrier = pltpu.get_barrier_semaphore()
+    partners = others + [(me, p * CORES + core) for p in across] + [mate]
+    for partner in partners:
+        pl.semaphore_signal(barrier, inc=1, device_id=partner, device_id_type=MESH)
+
+    def remote(src, dst, send_sem, recv_sem, device):
+        return pltpu.make_async_remote_copy(
+            src_ref=src,
+            dst_ref=dst,
+            send_sem=send_sem,
+            recv_sem=recv_sem,
+            device_id=device,
+            device_id_type=MESH,
+        )
+
+    def piece(block, side, kind, device):
+        rows = rows_all.at[block, pl.ds(pl.multiple_of(side * half, half), half)]
+        return remote(
+            rows,
+            rows,
+            rows_send.at[block * kinds + kind],
+            rows_recv.at[block * CORES + side],
+            device,
+        )
+
+    def to_z(block, kind):
+        return piece(block, core, kind, (me - ny if kind == 0 else me + ny, group))
+
+    def to_y(block):
+        return [
+            piece(block, core, 3 + k - 1, (z * ny + lax.rem(y + k, ny), group))
+            for k in range(1, ny)
+        ]
+
+    def to_mate(block):
+        return piece(block, core, 2, mate)
+
+    def walk_z(k, act):
+        @pl.when(z + k < nz)
+        def from_above():
+            block = me + k * ny
+            act(block, 0, z > 0)
+
+        @pl.when(z - k >= 0)
+        def from_below():
+            block = me - k * ny
+            act(block, 1, z < nz - 1)
+
+    def relay(block, kind, onward):
+        to_mate(block).wait_recv()
+
+        @pl.when(onward)
+        def pass_on():
+            to_z(block, kind).start()
+
+        for copy in to_y(block):
+            copy.start()
+        to_mate(block).start()
+
+    def drain(block, kind, onward):
+        @pl.when(onward)
+        def sent():
+            to_z(block, kind).wait_send()
+
+        for copy in to_y(block):
+            copy.wait_send()
+        to_mate(block).wait_send()
+
+    def walk_y(k, act):
+        for j in range(1, ny):
+            column = lax.rem(y + j, ny)
+            if k == 0:
+                act(z * ny + column)
+            else:
+
+                @pl.when(z + k < nz)
+                def above():
+                    act((z + k) * ny + column)
+
+                @pl.when(z - k >= 0)
+                def below():
+                    act((z - k) * ny + column)
+
+    def share_y(block):
+        to_mate(block).wait_recv()
+        to_mate(block).start()
+
+    def mix(rows, sample):
+        fraction = frac_ref[sample]
+        anchor = clean_ref[rows].astype(jnp.float32)
+        drift = noise_ref[rows].astype(jnp.float32)
+        return (1.0 - fraction) * anchor + fraction * drift, drift - anchor
+
+    def modulate_rows(base):
+        def step(i, carry):
+            first = pl.multiple_of(base + i * CHUNK, CHUNK)
+            rows = pl.ds(first, CHUNK)
+            sample = first // rows_per
+            noisy, unused = mix(rows, sample)
+            centred = noisy - jnp.mean(noisy, -1, keepdims=True)
+            variance = jnp.mean(centred * centred, -1, keepdims=True)
+            normed = centred * lax.rsqrt(variance + 1e-06)
+            shift = modulation_ref[pl.ds(sample, 1), :features]
+            scale = modulation_ref[pl.ds(sample, 1), features : 2 * features]
+            rows_all[me, rows] = (normed * (1.0 + scale) + shift).astype(jnp.bfloat16)
+            return carry
+
+        lax.fori_loop(0, half // CHUNK, step, 0)
+
+    modulate_rows(core * half)
+    modulate_rows((1 - core) * half)
+    pl.semaphore_wait(barrier, len(partners))
+
+    @pl.when(z > 0)
+    def first_down():
+        to_z(me, 0).start()
+
+    @pl.when(z < nz - 1)
+    def first_up():
+        to_z(me, 1).start()
+
+    for copy in to_y(me):
+        copy.start()
+
+    preact[:, (units // LANES) * LANES :] = jnp.zeros(
+        (preact.shape[0], preact.shape[1] - (units // LANES) * LANES), jnp.float32
+    )
+    load_up.wait()
+    preact[:, :units] = jnp.dot(rows_all[me], up[...], preferred_element_type=jnp.float32)
+    values = preact[:, :units]
+    hidden[...] = jax.nn.gelu(values, approximate=True).astype(jnp.bfloat16)
+    load_down.wait()
+    part_out[...] = jnp.dot(
+        hidden[mate_rows], down[...], preferred_element_type=jnp.float32
+    ).astype(jnp.bfloat16)
+    part_copy = remote(part_out, part_in, part_sem.at[0], part_sem.at[1], mate)
+    part_copy.start()
+    part_own[...] = jnp.dot(hidden[own_rows], down[...], preferred_element_type=jnp.float32)
+    part_copy.wait_recv()
+    chip_sum[x] = (part_own[...] + part_in[...].astype(jnp.float32)).astype(jnp.bfloat16)
+    chip_copies = [
+        remote(
+            chip_sum.at[x],
+            chip_sum.at[x],
+            chip_send.at[p],
+            chip_recv.at[x],
+            (me, p * CORES + core),
+        )
+        for p in across
+    ]
+    for copy in chip_copies:
+        copy.start()
+
+    for j in range(preact.shape[1] // LANES):
+        block = preact[:, j * LANES : (j + 1) * LANES]
+        slope_t[j * LANES : (j + 1) * LANES, :] = gelu_slope(block).T
+
+    if nz > 1:
+        walk_z(1, relay)
+
+    for p in across:
+        remote(
+            chip_sum.at[p], chip_sum.at[p], chip_send.at[p], chip_recv.at[p], mate
+        ).wait_recv()
+
+    scale_all = loss_scale * 2.0 / (rows_per * features)
+
+    def slope_step(i, total):
+        first = pl.multiple_of(core * half + i * CHUNK, CHUNK)
+        rows = pl.ds(first, CHUNK)
+        here = pl.ds(pl.multiple_of(i * CHUNK, CHUNK), CHUNK)
+        sample = first // rows_per
+        noisy, target = mix(rows, sample)
+        output = chip_sum[0, here].astype(jnp.float32)
+        for p in range(1, nx):
+            output = output + chip_sum[p, here].astype(jnp.float32)
+        gate = modulation_ref[pl.ds(sample, 1), 2 * features :]
+        errors = noisy + gate * output - target
+        weight = weight_ref[sample]
+        slopes[rows] = (scale_all * weight * gate * errors).astype(jnp.bfloat16)
+        return total + weight * jnp.sum(errors * errors, -1, keepdims=True)
+
+    squares = lax.fori_loop(0, half // CHUNK, slope_step, jnp.zeros((CHUNK, 1), jnp.float32))
+    own_slopes = slopes.at[own_rows]
+    slopes_copy = remote(own_slopes, own_slopes, slopes_sem.at[0], slopes_sem.at[1], mate)
+    slopes_copy.start()
+    loss_part = jnp.sum(squares) / (rows_per * features)
+    core_tile[core] = jnp.full((8, LANES), loss_part, jnp.float32)
+    core_copy = remote(
+        core_tile.at[core], core_tile.at[core], core_sem.at[0], core_sem.at[1], mate
+    )
+    core_copy.start()
+    slopes_copy.wait_recv()
+
+    slope_all = lax.dot_general(
+        down[...], slopes[...], (((1,), (1,)), ((), ())), preferred_element_type=jnp.float32
+    )
+    for d in range(ndp):
+        part = slice(d * share, (d + 1) * share)
+        pre_out[d] = (slope_all[part] * slope_t[part, :]).astype(jnp.bfloat16)
+    pre_in[me] = pre_out[me]
+    pre_copies = [
+        remote(pre_out.at[peer[0]], pre_in.at[me], pre_send.at[peer[0]], pre_recv.at[me], peer)
+        for peer in others
+    ]
+    for copy in pre_copies:
+        copy.start()
+
+    core_copy.wait_recv()
+    weight_here = weight_ref[0]
+    for sample in range(1, samples):
+        weight_here = weight_here + weight_ref[sample]
+    line = lax.broadcasted_iota(jnp.int32, (8, LANES), 0)
+    all_tile[me] = jnp.where(line == 0, core_tile[0] + core_tile[1], weight_here)
+    tile_copies = [
+        remote(all_tile.at[me], all_tile.at[me], tile_send.at[peer[0]], tile_recv.at[me], peer)
+        for peer in others
+    ]
+    for copy in tile_copies:
+        copy.start()
+
+    walk_y(0, share_y)
+    for k in range(2, nz):
+        walk_y(k - 1, share_y)
+        walk_z(k, relay)
+    if nz > 1:
+        walk_y(nz - 1, share_y)
+
+    grad_ref[...] = jnp.dot(pre_in[me], rows_all[me], preferred_element_type=jnp.float32)
+
+    def grad_step(k, carry):
+        block = lax.rem(me + k, ndp)
+        piece(block, 1 - core, 2, mate).wait_recv()
+        remote(
+            pre_out.at[block], pre_in.at[block], pre_send.at[block], pre_recv.at[block], mate
+        ).wait_recv()
+        grad_ref[...] += jnp.dot(
+            pre_in[block], rows_all[block], preferred_element_type=jnp.float32
+        )
+        return carry
+
+    lax.fori_loop(1, ndp, grad_step, 0)
+
+    for peer in others:
+        block = peer[0]
+        remote(
+            all_tile.at[block], all_tile.at[block], tile_send.at[block], tile_recv.at[block], peer
+        ).wait_recv()
+    sums = all_tile[0]
+    for d in range(1, ndp):
+        sums = sums + all_tile[d]
+    sums_ref[...] = sums
+
+    @pl.when(z > 0)
+    def first_down_sent():
+        to_z(me, 0).wait_send()
+
+    @pl.when(z < nz - 1)
+    def first_up_sent():
+        to_z(me, 1).wait_send()
+
+    for copy in to_y(me) + [part_copy, slopes_copy, core_copy]:
+        copy.wait_send()
+    for copy in chip_copies + pre_copies + tile_copies:
+        copy.wait_send()
+    for k in range(1, nz):
+        walk_z(k, drain)
+    for k in range(nz):
+        walk_y(k, lambda block: to_mate(block).wait_send())
+
+
+def local_kernel(sizes, clean, noise, modulation, strata, up_weight, down_weight):
+    samples_here, rows_per, features = clean.shape
+    nz, ny, nx = sizes
+    ndp, tokens, units = nz * ny, samples_here * rows_per, up_weight.shape[1]
+    half, share, padded = tokens // CORES, units // ndp, pl.cdiv(units, LANES) * LANES
+    fraction, weight = stratum_weights(strata)
+    bf16, f32 = jnp.bfloat16, jnp.float32
+    vmem = pl.BlockSpec(memory_space=pltpu.VMEM)
+    smem = pl.BlockSpec(memory_space=pltpu.SMEM)
+    anywhere = pl.BlockSpec(memory_space=pl.ANY)
+    dma = pltpu.SemaphoreType.DMA
+    gradient, sums = pl.pallas_call(
+        functools.partial(step_kernel, (nz, ny, nx, rows_per)),
+        out_shape=(
+            jax.ShapeDtypeStruct((share, features), f32),
+            jax.ShapeDtypeStruct((8, LANES), f32),
+        ),
+        in_specs=[smem, smem, vmem, vmem, vmem, anywhere, anywhere],
+        out_specs=(vmem, vmem),
+        scratch_shapes=[
+            pltpu.VMEM((features, units), bf16),
+            pltpu.VMEM((units, features), bf16),
+            pltpu.VMEM((ndp, tokens, features), bf16),
+            pltpu.VMEM((tokens, padded), f32),
+            pltpu.VMEM((padded, tokens), f32),
+            pltpu.VMEM((tokens, units), bf16),
+            pltpu.VMEM((half, features), bf16),
+            pltpu.VMEM((half, features), bf16),
+            pltpu.VMEM((half, features), f32),
+            pltpu.VMEM((nx, half, features), bf16),
+            pltpu.VMEM((tokens, features), bf16),
+            pltpu.VMEM((ndp, share, tokens), bf16),
+            pltpu.VMEM((ndp, share, tokens), bf16),
+            pltpu.VMEM((CORES, 8, LANES), f32),
+            pltpu.VMEM((ndp, 8, LANES), f32),
+            dma((2,)),
+            dma((ndp * (2 + ny),)),
+            dma((ndp * CORES,)),
+            dma((2,)),
+            dma((nx,)),
+            dma((nx,)),
+            dma((2,)),
+            dma((2,)),
+            dma((ndp,)),
+            dma((ndp,)),
+            dma((ndp,)),
+            dma((ndp,)),
+        ],
+        compiler_params=pltpu.CompilerParams(
+            collective_id=0, has_side_effects=True, vmem_limit_bytes=60 * 1024 * 1024
+        ),
+    )(
+        fraction,
+        weight,
+        clean.reshape(tokens, features),
+        noise.reshape(tokens, features),
+        modulation,
+        up_weight,
+        down_weight,
+    )
+    return (gradient / sums[1, 0], sums[0, 0] / sums[1, 0])
+
+
+def chip_sizes(mesh):
+    if mesh.shape["mp"] % CORES:
+        return None
+    spots = [tuple(d.coords) for d in mesh.devices[:, 0]]
+    ny = len({spot[1] for spot in spots})
+    return (mesh.shape["dp"] // ny, ny, mesh.shape["mp"] // CORES)
+
+
+def local(sizes, clean, *others):
     gathered = lax.axis_size("dp") * clean.size * clean.dtype.itemsize
-    body = local_gather if gathered <= GATHER_LIMIT_BYTES else local_scatter
-    return body(clean, *others)
+    units = others[-1].shape[0]
+    half = clean.shape[0] * clean.shape[1] // CORES
+    if gathered > GATHER_LIMIT_BYTES:
+        return local_scatter(clean, *others)
+    if units % (8 * lax.axis_size("dp")) or half % LANES or clean.shape[1] % CHUNK:
+        return local_gather(clean, *others)
+    return local_kernel(sizes, clean, *others)
 
 
 def solution(mesh):
     return jax.shard_map(
-        local,
+        functools.partial(local, chip_sizes(mesh)),
         mesh=mesh,
         in_specs=(
             P("dp", None, None),

time: 200 us -> 108 us (0.54)
  waiting for transfers between devices: 104 us -> 0 us
  Pallas kernels: 0 us -> 88.7 us
  blocking collectives: 32.5 us -> 0 us
  matrix products: 25.9 us -> 0 us
  between operations: 18 us -> 3.09 us
  local copies, waits for them, and re-layouts: 1.01 us -> 11.2 us
  other arithmetic: 11.9 us -> 4.57 us
  starting transfers between devices: 5.58 us -> 0 us
    pallas_call x0 -> x1, Pallas kernels: none -> 88.7 us  [local_kernel(): pl.pallas_call(functools.partial(step_kernel, (nz, ny, nx, rows_per)), ou...]
    all_gather x1 -> x0, waiting for transfers between devices: 63.1 us -> none  [local_gather(): every_row = lax.all_gather(flat_rows, 'dp', axis=0, tiled=True)]
    psum x1 -> x0, waiting for transfers between devices: 40.6 us -> none  [local_gather(): lax.psum(partial_value.astype(jnp.bfloat16), 'mp').astype(jnp.float32)]
    psum x1 -> x0, blocking collectives: 32.5 us -> none  [local_gather(): lax.psum(jnp.stack([jnp.sum(weight * squares), jnp.sum(weight)]), 'dp')]
    dot_general x4 -> x0, matrix products: 25.9 us -> none  [the longest x1 7.51 us: local_gather(): lax.dot_general(own_slope, every_row, (((0,), (0,)), ((), ())), preferred...]
    unnamed x12 -> x1, local copies, waits for them, and re-layouts: 0.36 us -> 9.91 us
    reduce_sum x4 -> x0, other arithmetic: 6.22 us -> none  [the longest x1 2.51 us: local_gather(): squares = jnp.sum(errors * errors, axis=(1, 2)) / (rows_per * features)]
    all_to_all x1 -> x0, starting transfers between devices: 5.5 us -> none  [local_gather(): lax.all_to_all(pre_slope, 'dp', split_axis=1, concat_axis=0, tiled=True)]
  transfers between devices with their start and end apart: 3 -> 0, of which waited for: 2 -> 0; matrix products, arithmetic and copies ran while one was open for 6% -> 0% of each run, Pallas kernels for 0% -> 0%
where the time goes in v2:
time: 108 us
  Pallas kernels  88.7 us (82%)
  local copies, waits for them, and re-layouts  11.2 us (10%)
  other arithmetic  4.57 us (4%)
  between operations  3.09 us (3%)
    pallas_call x1, Pallas kernels, local_kernel(): pl.pallas_call(functools.partial(step_kernel, (nz, ny, nx, rows_per)), ou...  88.7 us
    unnamed x1, local copies, waits for them, and re-layouts  9.91 us
    div x1, other arithmetic, local_kernel(): return (gradient / sums[1, 0], sums[0, 0] / sums[1, 0])  3.33 us

profile of v2, /device:TPU:0, one launch (start us, length us, event | category | flops | bytes accessed | tf_op | source)
XLA Modules:
  0.0 107.6 jit_solution(4705619697161345297)
XLA Ops:
  0.6 1.2 %multiply_divide_fusion = (f32[2]{0:T(128)}, f32[2]{0:T(128)}) fusion(s32[2]{0:T(128)} %param.9), kind=kLoop, calls=%fused_computation.5 | loop fusion | flops 102 | bytes 24 | tf_op jit(solution)/shard_map/div | solution.py:21
  1.9 9.9 %copy.8.up_hbm = bf16[2432,1344]{1,0:T(8,128)(2,1)} copy(bf16[2432,1344]{0,1:T(8,128)(2,1)} %param.10) | data formatting | bytes 13074432 | tf_op args[4]
  11.8 88.7 %shard_map.77 = (f32[168,2432]{1,0:T(8,128)}, f32[8,128]{1,0:T(8,128)}) custom-call(f32[2]{0:T(128)} %get-tuple-element.7.frac_ref, f32[2]{0:T(128)} %get-tuple-element.6.weight_ref, bf16[256,2432]{1,0:T(8,128)(2,1)} %bitcast.4, bf16[256,2432]{1,0:T(8,128)(2,1)} %bitcast.5, f32[2,7296]{1,0:T(2,128)} %modulation_ref.1, bf16[2432,1344]{1,0:T(8,128)(2,1)} %copy.8.up_hbm, ...), custom_call_target="tpu_custom_call" | custom-call | tf_op jit(solution)/shard_map/pallas_call | solution.py:485
  100.4 1.3 %fusion.2 = (f32[1,1]{1,0:T(1,128)}, f32[1,1]{1,0:T(1,128)}) fusion(f32[8,128]{1,0:T(8,128)} %get-tuple-element.5), kind=kLoop, calls=%fused_computation.9 | loop fusion | bytes 16 | tf_op jit(solution)/shard_map/slice | solution.py:534
  103.1 3.3 %broadcast_divide_fusion = f32[168,2432]{1,0:T(8,128)} fusion(f32[168,2432]{1,0:T(8,128)} %get-tuple-element.4, f32[]{:T(128)} %bitcast.2), kind=kLoop, calls=%fused_computation | loop fusion | flops 408576 | bytes 3268612 | tf_op jit(solution)/shard_map/div | solution.py:534

commit v3 on v2

--- a/solution.py
+++ b/solution.py
@@ -182,10 +182,11 @@
     nz, ny, nx, rows_per = sizes
     ndp = nz * ny
     samples, features = clean_ref.shape[0] // rows_per, clean_ref.shape[1]
-    units = up.shape[1]
+    units = up.shape[0]
     half = clean_ref.shape[0] // CORES
     share = units // ndp
-    kinds = 3 + (ny - 1)
+    strip = half // nx
+    kinds = 2 + CORES * nx + (ny - 1) + (nx - 1)
     me, group = lax.axis_index("dp"), lax.axis_index("mp")
     z, y = me // ny, lax.rem(me, ny)
     x, core = group // CORES, lax.rem(group, CORES)
@@ -215,38 +216,55 @@
             device_id_type=MESH,
         )
 
-    def piece(block, side, kind, device):
-        rows = rows_all.at[block, pl.ds(pl.multiple_of(side * half, half), half)]
+    mate_kind, y_kind = 2, 2 + nx
+    x_kind = y_kind + ny - 1
+
+    def copy_rows(block, first, count, kind, arrival, device):
+        rows = rows_all.at[block, pl.ds(pl.multiple_of(first, count), count)]
         return remote(
             rows,
             rows,
             rows_send.at[block * kinds + kind],
-            rows_recv.at[block * CORES + side],
+            rows_recv.at[block * CORES * nx + arrival],
             device,
         )
 
+    def piece(block, side, kind, device):
+        return copy_rows(block, side * half, half, kind, side * nx, device)
+
+    def strip_of(block, side, lane, kind, device):
+        first = side * half + lane * strip
+        return copy_rows(block, first, strip, kind, side * nx + lane, device)
+
     def to_z(block, kind):
         return piece(block, core, kind, (me - ny if kind == 0 else me + ny, group))
 
     def to_y(block):
         return [
-            piece(block, core, 3 + k - 1, (z * ny + lax.rem(y + k, ny), group))
+            strip_of(block, core, x, y_kind + k - 1, (z * ny + lax.rem(y + k, ny), group))
             for k in range(1, ny)
         ]
 
+    def to_x(block):
+        return [
+            strip_of(block, core, x, x_kind + k - 1, (me, lax.rem(x + k, nx) * CORES + core))
+            for k in range(1, nx)
+        ]
+
     def to_mate(block):
-        return piece(block, core, 2, mate)
+        return piece(block, core, mate_kind, mate)
+
+    def strip_to_mate(block, lane):
+        return strip_of(block, core, lane, mate_kind + lane, mate)
 
     def walk_z(k, act):
         @pl.when(z + k < nz)
         def from_above():
-            block = me + k * ny
-            act(block, 0, z > 0)
+            act(me + k * ny, 0, z > 0)
 
         @pl.when(z - k >= 0)
         def from_below():
-            block = me - k * ny
-            act(block, 1, z < nz - 1)
+            act(me - k * ny, 1, z < nz - 1)
 
     def relay(block, kind, onward):
         to_mate(block).wait_recv()
@@ -284,8 +302,28 @@
                     act((z - k) * ny + column)
 
     def share_y(block):
-        to_mate(block).wait_recv()
-        to_mate(block).start()
+        strip_to_mate(block, x).wait_recv()
+        for copy in to_x(block):
+            copy.start()
+        strip_to_mate(block, x).start()
+
+    def share_x(block):
+        for p in across:
+            strip_to_mate(block, p).wait_recv()
+            strip_to_mate(block, p).start()
+
+    def drain_y(block):
+        for copy in to_x(block):
+            copy.wait_send()
+        for lane in range(nx):
+            strip_to_mate(block, lane).wait_send()
+
+    def await_own_column(block):
+        piece(block, 1 - core, mate_kind, mate).wait_recv()
+
+    def await_other_column(block):
+        for lane in range(nx):
+            strip_of(block, 1 - core, lane, mate_kind, mate).wait_recv()
 
     def mix(rows, sample):
         fraction = frac_ref[sample]
@@ -324,20 +362,23 @@
     for copy in to_y(me):
         copy.start()
 
-    preact[:, (units // LANES) * LANES :] = jnp.zeros(
-        (preact.shape[0], preact.shape[1] - (units // LANES) * LANES), jnp.float32
-    )
+    tail = (units // LANES) * LANES
+    preact[tail:, :] = jnp.zeros((preact.shape[0] - tail, preact.shape[1]), jnp.float32)
     load_up.wait()
-    preact[:, :units] = jnp.dot(rows_all[me], up[...], preferred_element_type=jnp.float32)
-    values = preact[:, :units]
-    hidden[...] = jax.nn.gelu(values, approximate=True).astype(jnp.bfloat16)
+    preact[:units, :] = lax.dot_general(
+        up[...], rows_all[me], (((1,), (1,)), ((), ())), preferred_element_type=jnp.float32
+    )
+    for j in range(preact.shape[0] // LANES):
+        part = slice(j * LANES, (j + 1) * LANES)
+        values = jax.nn.gelu(preact[part, :], approximate=True)
+        hidden[:, part] = values.T.astype(jnp.bfloat16)
     load_down.wait()
     part_out[...] = jnp.dot(
-        hidden[mate_rows], down[...], preferred_element_type=jnp.float32
+        hidden[mate_rows, :units], down[...], preferred_element_type=jnp.float32
     ).astype(jnp.bfloat16)
     part_copy = remote(part_out, part_in, part_sem.at[0], part_sem.at[1], mate)
     part_copy.start()
-    part_own[...] = jnp.dot(hidden[own_rows], down[...], preferred_element_type=jnp.float32)
+    part_own[...] = jnp.dot(hidden[own_rows, :units], down[...], preferred_element_type=jnp.float32)
     part_copy.wait_recv()
     chip_sum[x] = (part_own[...] + part_in[...].astype(jnp.float32)).astype(jnp.bfloat16)
     chip_copies = [
@@ -353,9 +394,7 @@
     for copy in chip_copies:
         copy.start()
 
-    for j in range(preact.shape[1] // LANES):
-        block = preact[:, j * LANES : (j + 1) * LANES]
-        slope_t[j * LANES : (j + 1) * LANES, :] = gelu_slope(block).T
+    slope_t[...] = gelu_slope(preact[...])
 
     if nz > 1:
         walk_z(1, relay)
@@ -423,16 +462,27 @@
 
     walk_y(0, share_y)
     for k in range(2, nz):
+        walk_z(k, relay)
         walk_y(k - 1, share_y)
-        walk_z(k, relay)
+        walk_y(k - 2, share_x)
     if nz > 1:
         walk_y(nz - 1, share_y)
+        walk_y(nz - 2, share_x)
+    walk_y(nz - 1, share_x)
 
     grad_ref[...] = jnp.dot(pre_in[me], rows_all[me], preferred_element_type=jnp.float32)
 
     def grad_step(k, carry):
         block = lax.rem(me + k, ndp)
-        piece(block, 1 - core, 2, mate).wait_recv()
+
+        @pl.when(lax.rem(block, ny) == y)
+        def own_column():
+            await_own_column(block)
+
+        @pl.when(lax.rem(block, ny) != y)
+        def other_column():
+            await_other_column(block)
+
         remote(
             pre_out.at[block], pre_in.at[block], pre_send.at[block], pre_recv.at[block], mate
         ).wait_recv()
@@ -451,7 +501,9 @@
     sums = all_tile[0]
     for d in range(1, ndp):
         sums = sums + all_tile[d]
-    sums_ref[...] = sums
+    loss_sum, weight_sum = sums[0, 0], sums[1, 0]
+    grad_ref[...] = grad_ref[...] / weight_sum
+    sums_ref[0, 0] = loss_sum / weight_sum
 
     @pl.when(z > 0)
     def first_down_sent():
@@ -468,7 +520,7 @@
     for k in range(1, nz):
         walk_z(k, drain)
     for k in range(nz):
-        walk_y(k, lambda block: to_mate(block).wait_send())
+        walk_y(k, drain_y)
 
 
 def local_kernel(sizes, clean, noise, modulation, strata, up_weight, down_weight):
@@ -482,21 +534,21 @@
     smem = pl.BlockSpec(memory_space=pltpu.SMEM)
     anywhere = pl.BlockSpec(memory_space=pl.ANY)
     dma = pltpu.SemaphoreType.DMA
-    gradient, sums = pl.pallas_call(
+    gradient, loss = pl.pallas_call(
         functools.partial(step_kernel, (nz, ny, nx, rows_per)),
         out_shape=(
             jax.ShapeDtypeStruct((share, features), f32),
-            jax.ShapeDtypeStruct((8, LANES), f32),
+            jax.ShapeDtypeStruct((1, 1), f32),
         ),
         in_specs=[smem, smem, vmem, vmem, vmem, anywhere, anywhere],
-        out_specs=(vmem, vmem),
+        out_specs=(vmem, smem),
         scratch_shapes=[
-            pltpu.VMEM((features, units), bf16),
+            pltpu.VMEM((units, features), bf16),
             pltpu.VMEM((units, features), bf16),
             pltpu.VMEM((ndp, tokens, features), bf16),
-            pltpu.VMEM((tokens, padded), f32),
             pltpu.VMEM((padded, tokens), f32),
-            pltpu.VMEM((tokens, units), bf16),
+            pltpu.VMEM((padded, tokens), f32),
+            pltpu.VMEM((tokens, padded), bf16),
             pltpu.VMEM((half, features), bf16),
             pltpu.VMEM((half, features), bf16),
             pltpu.VMEM((half, features), f32),
@@ -507,8 +559,8 @@
             pltpu.VMEM((CORES, 8, LANES), f32),
             pltpu.VMEM((ndp, 8, LANES), f32),
             dma((2,)),
-            dma((ndp * (2 + ny),)),
-            dma((ndp * CORES,)),
+            dma((ndp * (CORES * nx + ny + nx),)),
+            dma((ndp * CORES * nx,)),
             dma((2,)),
             dma((nx,)),
             dma((nx,)),
@@ -528,10 +580,10 @@
         clean.reshape(tokens, features),
         noise.reshape(tokens, features),
         modulation,
-        up_weight,
+        up_weight.T,
         down_weight,
     )
-    return (gradient / sums[1, 0], sums[0, 0] / sums[1, 0])
+    return (gradient, loss.reshape(()))
 
 
 def chip_sizes(mesh):
@@ -548,7 +600,7 @@
     half = clean.shape[0] * clean.shape[1] // CORES
     if gathered > GATHER_LIMIT_BYTES:
         return local_scatter(clean, *others)
-    if units % (8 * lax.axis_size("dp")) or half % LANES or clean.shape[1] % CHUNK:
+    if units % (8 * lax.axis_size("dp")) or half % (LANES // 2 * (lax.axis_size("mp") // CORES)) or clean.shape[1] % CHUNK:
         return local_gather(clean, *others)
     return local_kernel(sizes, clean, *others)
 

time: 108 us -> 93.1 us (0.86)
  local copies, waits for them, and re-layouts: 11.2 us -> 2.7 us
  other arithmetic: 4.57 us -> 1.23 us
  Pallas kernels: 88.7 us -> 86.5 us
    unnamed x1, local copies, waits for them, and re-layouts: 9.91 us -> 2.7 us
    div x1 -> x0, other arithmetic: 3.33 us -> none  [local_kernel(): return (gradient / sums[1, 0], sums[0, 0] / sums[1, 0])]
    pallas_call x1, Pallas kernels: 88.7 us -> 86.5 us  [local_kernel(): pl.pallas_call(functools.partial(step_kernel, (nz, ny, nx, rows_per)), ou...]
    slice x1 -> x0, local copies, waits for them, and re-layouts: 1.33 us -> none  [local_kernel(): return (gradient / sums[1, 0], sums[0, 0] / sums[1, 0])]
where the time goes in v3:
time: 93.1 us; the launch traced here: 92.9 us
  Pallas kernels  86.5 us (93%)
  local copies, waits for them, and re-layouts  2.7 us (3%)
  between operations  2.39 us (3%)
  other arithmetic  1.23 us (1%)
    pallas_call x1, Pallas kernels, local_kernel(): pl.pallas_call(functools.partial(step_kernel, (nz, ny, nx, rows_per)), ou...  86.5 us
    unnamed x1, local copies, waits for them, and re-layouts  2.7 us

profile of v3, /device:TPU:0, one launch (start us, length us, event | category | flops | bytes accessed | tf_op | source)
XLA Modules:
  0.0 92.9 jit_solution(685775220273747897)
XLA Ops:
  0.6 1.2 %multiply_divide_fusion = (f32[2]{0:T(128)}, f32[2]{0:T(128)}) fusion(s32[2]{0:T(128)} %param.9), kind=kLoop, calls=%fused_computation.4 | loop fusion | flops 102 | bytes 24 | tf_op jit(solution)/shard_map/div | solution.py:21
  1.9 86.5 %shard_map.77 = (f32[168,2432]{1,0:T(8,128)}, f32[1,1]{1,0:T(1,128)}) custom-call(f32[2]{0:T(128)} %get-tuple-element.7.frac_ref, f32[2]{0:T(128)} %get-tuple-element.6.weight_ref, bf16[256,2432]{1,0:T(8,128)(2,1)} %bitcast.5, bf16[256,2432]{1,0:T(8,128)(2,1)} %bitcast.6, f32[2,7296]{1,0:T(2,128)} %modulation_ref.1, bf16[1344,2432]{1,0:T(8,128)(2,1)} %bitcast.4, ...), custom_call_target="tpu_custom_call" | custom-call | tf_op jit(solution)/shard_map/pallas_call | solution.py:537
  88.4 2.7 %copy.10 = f32[168,2432]{1,0:T(8,128)} copy(f32[168,2432]{1,0:T(8,128)} %get-tuple-element.10) | data formatting | bytes 3268608
